TPU v7x, 32 devices: a whole 2x2x4 slice. The times are simulated.
32 devices in a mesh: seq: 8 (over y, x, core), head: 4 (over z).
Axes of the slice: x: 2, y: 2, z: 4, core: 2. Of those that a mesh axis runs over, the one named last changes fastest.
Arguments:
- tokens: bfloat16 [32, 1024, 1024], P('seq'), may hold values from -6 to 6
- w_query: bfloat16 [1024, 1024], P(None, 'head'), may hold values from -1 to 1
- w_key: bfloat16 [1024, 1024], P(None, 'head'), may hold values from -1 to 1
- w_value: bfloat16 [1024, 1024], P(None, 'head'), may hold values from -0.1875 to 0.1875
- w_out: bfloat16 [1024, 1024], P('head'), may hold values from -0.1875 to 0.1875
Outputs:
- mixed: bfloat16 [32, 1024, 1024], P('seq', None, 'head')
All inputs are finite; a program needn't handle non-finite values.
Results may differ from a plain program's by a relative error of at most 0.012.
Values may be sent and summed in bfloat16 or wider, within the bound.
No kernel may reach another device: no remote copies, remote signals or barrier semaphores. Data moves between devices by JAX's collectives and lax.ppermute only.
A program may use at most 128 MiB of HBM per device.

v0:
```python
import jax
import jax.numpy as jnp
from jax import lax
from jax.sharding import PartitionSpec as P

HS = 64
epsilon = 1e-05


def normalize(tokens):
    values = tokens.astype(jnp.float32)
    row_mean = jnp.mean(values, axis=-1, keepdims=True)
    centered = values - row_mean
    row_var = jnp.mean(centered * centered, axis=-1, keepdims=True)
    return (centered * lax.rsqrt(row_var + epsilon)).astype(jnp.bfloat16)


def project(source, weight):
    return jnp.einsum("fpd,dc->fpc", source, weight, preferred_element_type=jnp.float32).astype(
        jnp.bfloat16
    )


def attend(queries, key_rows, value_rows, head_count):
    frames, patch_count, feature_width = queries.shape
    head_size = feature_width // head_count
    query_flat = queries.reshape(frames, patch_count * head_count, head_size)
    key_flat = key_rows.reshape(frames, patch_count * head_count, head_size)
    value_flat = value_rows.reshape(frames, patch_count * head_count, head_size)
    scores = jnp.einsum(
        "fmd,gmd->fgm", query_flat, key_flat, preferred_element_type=jnp.float32
    ) * head_size ** (-0.5)
    row_top = jnp.max(scores, axis=1, keepdims=True)
    raised = jnp.exp(scores - row_top)
    weights = (raised / jnp.sum(raised, axis=1, keepdims=True)).astype(jnp.bfloat16)
    attended = jnp.einsum("fgm,gmd->fmd", weights, value_flat, preferred_element_type=jnp.float32)
    return attended.astype(jnp.bfloat16).reshape(frames, patch_count, feature_width)


def local(tokens, w_query, w_key, w_value, w_out):
    normed = normalize(tokens)
    head_count = w_query.shape[1] // HS
    local_query = project(normed, w_query)
    local_key = project(normed, w_key)
    local_value = project(normed, w_value)
    queries, key_rows, value_rows = (
        lax.all_to_all(local_query, "seq", split_axis=1, concat_axis=0, tiled=True),
        lax.all_to_all(local_key, "seq", split_axis=1, concat_axis=0, tiled=True),
        lax.all_to_all(local_value, "seq", split_axis=1, concat_axis=0, tiled=True),
    )
    attended = attend(queries, key_rows, value_rows, head_count)
    partial_value = jnp.einsum("fpc,cd->fpd", attended, w_out, preferred_element_type=jnp.float32)
    columns = lax.psum_scatter(
        partial_value.astype(jnp.bfloat16), "head", scatter_dimension=2, tiled=True
    )
    return lax.all_to_all(columns, "seq", split_axis=0, concat_axis=1, tiled=True)


def solution(mesh):
    return jax.shard_map(
        local,
        mesh=mesh,
        in_specs=(
            P("seq", None, None),
            P(None, "head"),
            P(None, "head"),
            P(None, "head"),
            P("head", None),
        ),
        out_specs=P("seq", None, "head"),
        check_vma=False,
    )
```

profile of v0, /device:TPU:0, one launch (start us, length us, event | category | flops | bytes accessed | tf_op | source)
XLA Modules:
  0.0 326.3 jit_solution(13314724638309537397)
XLA Ops:
  6.5 0.0 copy-start
  6.5 0.0 copy-start.1
  6.5 0.0 copy-start.3
  6.5 4.7 %convert_reduce_fusion = f32[4,1024]{1,0:T(4,128)S(1)} fusion(bf16[4,1024,1024]{2,1,0:T(8,128)(2,1)} %param.5), kind=kLoop, calls=%fused_computation.2 | loop fusion | flops 8384512 | bytes 8404992 | tf_op jit(solution)/shard_map/reduce_sum | solution.py:12
  11.3 1.1 copy-done.1
  12.4 2.8 fusion.3
  15.2 0.0 copy-done.3
  15.2 3.1 fusion.28
  18.3 0.0 copy-start.4
  18.4 3.0 copy.19
  21.3 5.2 %all-to-all-start.1 = ((bf16[4,1024,256]{2,0,1:T(4,128)(2,1)}), bf16[4,1024,256]{2,0,1:T(4,128)(2,1)S(1)}, u32[]{:S(2)}, u32[]{:S(2)}) async-start(bf16[4,1024,256]{2,0,1:T(4,128)(2,1)} %copy.19), calls=%async_computation.1 | async-start | bytes 4194304 | tf_op jit(solution)/shard_map/all_to_all | solution.py:48
  26.5 0.0 copy-done.4
  26.5 5.0 %fusion.31 = bf16[4,1024,256]{2,1,0:T(8,128)(2,1)S(1)} fusion(bf16[4,1024,1024]{2,1,0:T(8,128)(2,1)} %param.5, f32[4,1024]{1,0:T(4,128)S(1)} %add_rsqrt_fusion, f32[4,1024]{1,0:T(4,128)S(1)} %broadcast_multiply_fusion, bf16[1024,256]{1,0:T(8,128)(2,1)S(1)} %copy-done.4), kind=kOutput, calls=%fused_computation.30 | convolution fusion | flops 2165309440 | bytes 11042816 | tf_op jit(solution)/shard_map/fpd,dc->fpc/dot_general | solution.py:19
  31.5 0.0 copy-start.5
  31.6 2.9 copy.21
  34.5 18.6 %all-to-all-done.1 = bf16[4,1024,256]{2,0,1:T(4,128)(2,1)S(1)} async-done(((bf16[4,1024,256]{2,0,1:T(4,128)(2,1)}), bf16[4,1024,256]{2,0,1:T(4,128)(2,1)S(1)}, u32[]{:S(2)}, u32[]{:S(2)}) %all-to-all-start.1) | async-done | bytes 2097184 | tf_op jit(solution)/shard_map/all_to_all | solution.py:48
  53.1 0.0 copy-start.2
  53.1 4.3 %all-to-all-start.2 = ((bf16[4,1024,256]{2,0,1:T(4,128)(2,1)}), bf16[4,1024,256]{2,0,1:T(4,128)(2,1)}, u32[]{:S(2)}, u32[]{:S(2)}) async-start(bf16[4,1024,256]{2,0,1:T(4,128)(2,1)} %copy.21), calls=%async_computation.2 | async-start | bytes 4194304 | tf_op jit(solution)/shard_map/all_to_all | solution.py:47
  57.5 0.0 copy-done.5
  57.5 5.0 %fusion.25 = bf16[4,1024,256]{2,1,0:T(8,128)(2,1)S(1)} fusion(bf16[4,1024,1024]{2,1,0:T(8,128)(2,1)} %param.5, f32[4,1024]{1,0:T(4,128)S(1)} %add_rsqrt_fusion, f32[4,1024]{1,0:T(4,128)S(1)} %broadcast_multiply_fusion, bf16[1024,256]{1,0:T(8,128)(2,1)S(1)} %copy-done.5), kind=kOutput, calls=%fused_computation.28 | convolution fusion | flops 2165309440 | bytes 11042816 | tf_op jit(solution)/shard_map/fpd,dc->fpc/dot_general | solution.py:19
  62.5 0.0 copy-done.2
  62.5 2.9 copy.17
  65.5 18.7 %all-to-all-done.2 = bf16[4,1024,256]{2,0,1:T(4,128)(2,1)} async-done(((bf16[4,1024,256]{2,0,1:T(4,128)(2,1)}), bf16[4,1024,256]{2,0,1:T(4,128)(2,1)}, u32[]{:S(2)}, u32[]{:S(2)}) %all-to-all-start.2) | async-done | bytes 2097184 | tf_op jit(solution)/shard_map/all_to_all | solution.py:47
  84.1 4.4 %all-to-all-start = ((bf16[4,1024,256]{2,0,1:T(4,128)(2,1)}), bf16[4,1024,256]{2,0,1:T(4,128)(2,1)}, u32[]{:S(2)}, u32[]{:S(2)}) async-start(bf16[4,1024,256]{2,0,1:T(4,128)(2,1)} %copy.17), calls=%async_computation | async-start | bytes 4194304 | tf_op jit(solution)/shard_map/all_to_all | solution.py:49
  88.5 0.2 reduce-scatter.2.cloned.1.call-start
  88.7 2.0 copy.42
  90.7 3.3 reshape.30
  94.0 2.0 copy.41
  95.9 3.2 reshape.31
  99.2 8.3 %fusion.18 = f32[512,32,32]{2,1,0:T(8,128)S(1)} fusion(bf16[32,512,64]{2,1,0:T(8,128)(2,1)} %reshape.31, bf16[32,512,64]{2,1,0:T(8,128)(2,1)} %reshape.30), kind=kOutput, calls=%fused_computation.19 | convolution fusion | flops 67108864 | bytes 6291456 | tf_op jit(solution)/shard_map/fmd,gmd->fgm/dot_general | solution.py:30
  107.5 6.1 %fusion.39 = (f32[32,512]{0,1:T(8,128)S(1)}, f32[32,32,512]{0,1,2:T(8,128)}) fusion(f32[512,32,32]{2,1,0:T(8,128)S(1)} %fusion.18), kind=kOutput, calls=%fused_computation.38 | output fusion | flops 2097183 | bytes 4259840 | tf_op jit(solution)/shard_map/sub | solution.py:34
  113.6 1.5 all-to-all-done
  115.1 2.0 copy.43
  117.1 3.3 %reshape.29 = bf16[32,512,64]{2,1,0:T(8,128)(2,1)} reshape(bf16[8,4,128,256]{3,2,1,0:T(8,128)(2,1)S(1)} %bitcast.50) | data formatting | bytes 4194304 | tf_op jit(solution)/shard_map/reshape | solution.py:29
  120.4 8.1 %convert_bitcast_fusion = bf16[32,512,64]{2,0,1:T(8,128)(2,1)S(1)} fusion(f32[32,32,512]{0,1,2:T(8,128)} %get-tuple-element.6, f32[32,512]{0,1:T(8,128)S(1)} %get-tuple-element.5, bf16[32,512,64]{2,1,0:T(8,128)(2,1)} %reshape.29), kind=kOutput, calls=%fused_computation.22 | convolution fusion | flops 69206016 | bytes 6356992 | tf_op jit(solution)/shard_map/fgm,gmd->fmd/dot_general | solution.py:36
  128.5 3.6 %copy.27 = bf16[32,512,64]{2,1,0:T(8,128)(2,1)} copy(bf16[32,512,64]{2,0,1:T(8,128)(2,1)S(1)} %convert_bitcast_fusion) | data formatting | bytes 4194304 | tf_op jit(solution)/shard_map/convert_element_type | solution.py:37
  132.1 5.5 %reshape.32 = bf16[32,128,256]{2,1,0:T(8,128)(2,1)S(1)} reshape(bf16[32,512,64]{2,1,0:T(8,128)(2,1)} %copy.27) | data formatting | bytes 4194304 | tf_op jit(solution)/shard_map/reshape | solution.py:37
  137.6 0.0 copy-done
  137.6 5.6 %convolution_convert_fusion = bf16[32,128,1024]{2,1,0:T(8,128)(2,1)} fusion(bf16[32,128,256]{2,1,0:T(8,128)(2,1)S(1)} %reshape.32, bf16[256,1024]{1,0:T(8,128)(2,1)S(1)} %copy-done), kind=kOutput, calls=%fused_computation.13 | convolution fusion | flops 2151677952 | bytes 11010048 | tf_op jit(solution)/shard_map/fpc,cd->fpd/dot_general | solution.py:52
  143.1 0.0 reduce-scatter.2.cloned.1.call-update
  143.2 144.7 %reduce-scatter.2.cloned.1.call-done = bf16[32,128,256]{2,1,0:T(8,128)(2,1)} async-done(((bf16[32,128,1024]{2,1,0:T(8,128)(2,1)}), bf16[32,128,256]{2,1,0:T(8,128)(2,1)}) %reduce-scatter.2.cloned.1.call-update) | async-done | bytes 2097168 | tf_op jit(solution)/shard_map/reduce_scatter | solution.py:53
  287.8 30.2 %all_to_all.63 = bf16[32,128,256]{2,1,0:T(8,128)(2,1)S(1)} all-to-all(bf16[32,128,256]{2,1,0:T(8,128)(2,1)} %reduce-scatter.2.cloned.1.call-done), channel_id=1, replica_groups=mesh['seq'=8,'head'=4] {'seq'}, dimensions={0} | all-to-all | bytes 4194304 | tf_op jit(solution)/shard_map/all_to_all | solution.py:56
  318.0 1.5 copy.28
  (2 shorter events, 0.0 us)
Async XLA Ops:
  6.5 131.0 %copy-start = (bf16[256,1024]{1,0:T(8,128)(2,1)S(1)}, bf16[256,1024]{1,0:T(8,128)(2,1)}, u32[]{:S(2)}) copy-start(bf16[256,1024]{1,0:T(8,128)(2,1)} %param.9) | copy-start | bytes 1572868
  6.5 5.8 %copy-start.1 = (bf16[4,1024,1024]{2,1,0:T(8,128)(2,1)S(1)}, bf16[4,1024,1024]{2,1,0:T(8,128)(2,1)}, u32[]{:S(2)}) copy-start(bf16[4,1024,1024]{2,1,0:T(8,128)(2,1)} %param.5) | copy-start | bytes 25165828
  6.5 8.6 %copy-start.3 = (bf16[1024,256]{1,0:T(8,128)(2,1)S(1)}, bf16[1024,256]{1,0:T(8,128)(2,1)}, u32[]{:S(2)}) copy-start(bf16[1024,256]{1,0:T(8,128)(2,1)} %param.7) | copy-start | bytes 1572868
  18.3 8.2 %copy-start.4 = (bf16[1024,256]{1,0:T(8,128)(2,1)S(1)}, bf16[1024,256]{1,0:T(8,128)(2,1)}, u32[]{:S(2)}) copy-start(bf16[1024,256]{1,0:T(8,128)(2,1)} %param.6) | copy-start | bytes 1572868
  21.3 31.8 %all-to-all-start.1 = ((bf16[4,1024,256]{2,0,1:T(4,128)(2,1)}), bf16[4,1024,256]{2,0,1:T(4,128)(2,1)S(1)}, u32[]{:S(2)}, u32[]{:S(2)}) async-start(bf16[4,1024,256]{2,0,1:T(4,128)(2,1)} %copy.19), calls=%async_computation.1 | async-start | bytes 4194304 | tf_op jit(solution)/shard_map/all_to_all | solution.py:48
  31.5 25.9 %copy-start.5 = (bf16[1024,256]{1,0:T(8,128)(2,1)S(1)}, bf16[1024,256]{1,0:T(8,128)(2,1)}, u32[]{:S(2)}) copy-start(bf16[1024,256]{1,0:T(8,128)(2,1)} %param.8) | copy-start | bytes 1572868
  53.1 9.4 %copy-start.2 = (bf16[4,1024,256]{2,0,1:T(4,128)(2,1)}, bf16[4,1024,256]{2,0,1:T(4,128)(2,1)S(1)}, u32[]{:S(2)}) copy-start(bf16[4,1024,256]{2,0,1:T(4,128)(2,1)S(1)} %all-to-all-done.1) | copy-start | bytes 6291460
  53.1 31.0 %all-to-all-start.2 = ((bf16[4,1024,256]{2,0,1:T(4,128)(2,1)}), bf16[4,1024,256]{2,0,1:T(4,128)(2,1)}, u32[]{:S(2)}, u32[]{:S(2)}) async-start(bf16[4,1024,256]{2,0,1:T(4,128)(2,1)} %copy.21), calls=%async_computation.2 | async-start | bytes 4194304 | tf_op jit(solution)/shard_map/all_to_all | solution.py:47
  84.1 31.0 %all-to-all-start = ((bf16[4,1024,256]{2,0,1:T(4,128)(2,1)}), bf16[4,1024,256]{2,0,1:T(4,128)(2,1)}, u32[]{:S(2)}, u32[]{:S(2)}) async-start(bf16[4,1024,256]{2,0,1:T(4,128)(2,1)} %copy.17), calls=%async_computation | async-start | bytes 4194304 | tf_op jit(solution)/shard_map/all_to_all | solution.py:49
  88.5 199.3 %reduce-scatter.2.cloned.1.call-start = ((), (), s32[]{:S(2)}) async-start(), calls=%async_computation.5 | async-start | bytes 10485760 | tf_op jit(solution)/shard_map/reduce_scatter | solution.py:53
Sparse Core Ops, SparseCore 0:
  143.3 144.4 reduce-scatter.1
where the time goes:
time: 327 us; the launch traced here: 326 us
  waiting for transfers between devices  184 us (56%)
  local copies, waits for them, and re-layouts  36.1 us (11%)
  matrix products  35.2 us (11%)
  blocking collectives  30.2 us (9%)
  starting transfers between devices  14.1 us (4%)
  other arithmetic  13.6 us (4%)
  between operations  13.6 us (4%)
    reduce_scatter x1, waiting for transfers between devices, local(): lax.psum_scatter(partial_value.astype(jnp.bfloat16), 'head', scatter_dime...  145 us
    all_to_all x1, blocking collectives, local(): lax.all_to_all(columns, 'seq', split_axis=0, concat_axis=1, tiled=True)  30.2 us
    all_to_all x1, waiting for transfers between devices, local(): lax.all_to_all(local_query, 'seq', split_axis=1, concat_axis=0, tiled=True)  18.7 us
    all_to_all x1, waiting for transfers between devices, local(): lax.all_to_all(local_key, 'seq', split_axis=1, concat_axis=0, tiled=True)  18.6 us
    dot_general x3, matrix products, project(): jnp.einsum('fpd,dc->fpc', source, weight, preferred_element_type=jnp.floa...  13.2 us
    convert_element_type x3, local copies, waits for them, and re-layouts, project(): jnp.einsum('fpd,dc->fpc', source, weight, preferred_element_type=jnp.floa...  8.83 us
    dot_general x1, matrix products, attend(): jnp.einsum('fmd,gmd->fgm', query_flat, key_flat, preferred_element_type=j...  8.29 us
    dot_general x1, matrix products, attend(): jnp.einsum('fgm,gmd->fmd', weights, value_flat, preferred_element_type=jn...  8.14 us
  transfers between devices with their start and end apart: 4, of which 4 were waited for; matrix products, arithmetic and copies ran while one was open for 12% of the time, Pallas kernels for 0%

commit v1 on v0

--- a/solution.py
+++ b/solution.py
@@ -5,6 +5,29 @@
 
 HS = 64
 epsilon = 1e-05
+
+
+def split_up(x, dim, size):
+    dims = x.shape
+    blocks = x.reshape(*dims[:dim], size, dims[dim] // size, *dims[dim + 1 :])
+    return jnp.moveaxis(blocks, dim, 0)
+
+
+def joined_along(tiles, dim):
+    tiles = jnp.moveaxis(tiles, 0, dim)
+    shape = tiles.shape
+    return tiles.reshape(*shape[:dim], shape[dim] * shape[dim + 1], *shape[dim + 2 :])
+
+
+def exchange_in_pairs(x, axis, split_dim, concat_dim):
+    peers, index = (lax.axis_size(axis), lax.axis_index(axis))
+    parts = split_up(x, split_dim, peers)
+    outs = [parts[index]]
+    for step in range(1, peers):
+        sent = parts[index ^ step]
+        outs.append(lax.ppermute(sent, axis, [(i, i ^ step) for i in range(peers)]))
+    parts = jnp.stack(outs)[index ^ jnp.arange(peers)]
+    return joined_along(parts, concat_dim)
 
 
 def normalize(tokens):
@@ -45,7 +68,7 @@
     local_value = project(normed, w_value)
     queries, key_rows, value_rows = (
         lax.all_to_all(local_query, "seq", split_axis=1, concat_axis=0, tiled=True),
-        lax.all_to_all(local_key, "seq", split_axis=1, concat_axis=0, tiled=True),
+        exchange_in_pairs(local_key, "seq", 1, 0),
         lax.all_to_all(local_value, "seq", split_axis=1, concat_axis=0, tiled=True),
     )
     attended = attend(queries, key_rows, value_rows, head_count)

time: 327 us -> 315 us (0.963)
  waiting for transfers between devices: 184 us -> 155 us
  local copies, waits for them, and re-layouts: 36.1 us -> 47 us
    all_to_all x1 -> x0, waiting for transfers between devices: 18.6 us -> none  [local(): lax.all_to_all(local_key, 'seq', split_axis=1, concat_axis=0, tiled=True)]
    all_to_all x1, waiting for transfers between devices: 18.7 us -> 7.12 us  [local(): lax.all_to_all(local_query, 'seq', split_axis=1, concat_axis=0, tiled=True)]
    unnamed x12 -> x19, local copies, waits for them, and re-layouts: 1.13 us -> 9.95 us
    ppermute x0 -> x7, starting transfers between devices: none -> 7.77 us  [exchange_in_pairs(): outs.append(lax.ppermute(sent, axis, [(i, i ^ step) for i in range(peers)]))]
    all_to_all x1 -> x0, starting transfers between devices: 5.21 us -> none  [local(): lax.all_to_all(local_key, 'seq', split_axis=1, concat_axis=0, tiled=True)]
    another operation x0 -> x2, local copies, waits for them, and re-layouts: none -> 4.91 us  [the longest x1 3.26 us: attend(): key_flat = key_rows.reshape(frames, patch_count * head_count, head_size)]
    ppermute x0 -> x7, waiting for transfers between devices: none -> 3.34 us  [exchange_in_pairs(): outs.append(lax.ppermute(sent, axis, [(i, i ^ step) for i in range(peers)]))]
    convert_element_type x3 -> x2, local copies, waits for them, and re-layouts: 8.83 us -> 7.5 us  [project(): jnp.einsum('fpd,dc->fpc', source, weight, preferred_element_type=jnp.floa...]
  transfers between devices with their start and end apart: 4 -> 10, of which waited for: 4 -> 4; matrix products, arithmetic and copies ran while one was open for 12% -> 17% of each run, Pallas kernels for 0% -> 0%
where the time goes in v1:
time: 315 us; the launch traced here: 314 us
  waiting for transfers between devices  155 us (49%)
  local copies, waits for them, and re-layouts  47 us (15%)
  matrix products  38.2 us (12%)
  blocking collectives  30.2 us (10%)
  starting transfers between devices  16.3 us (5%)
  other arithmetic  13.7 us (4%)
  between operations  13.6 us (4%)
    reduce_scatter x1, waiting for transfers between devices, local(): lax.psum_scatter(partial_value.astype(jnp.bfloat16), 'head', scatter_dime...  145 us
    all_to_all x1, blocking collectives, local(): lax.all_to_all(columns, 'seq', split_axis=0, concat_axis=1, tiled=True)  30.2 us
    dot_general x3, matrix products, project(): jnp.einsum('fpd,dc->fpc', source, weight, preferred_element_type=jnp.floa...  16.2 us
    unnamed x19, local copies, waits for them, and re-layouts  9.95 us
    dot_general x1, matrix products, attend(): jnp.einsum('fmd,gmd->fgm', query_flat, key_flat, preferred_element_type=j...  8.29 us
    dot_general x1, matrix products, attend(): jnp.einsum('fgm,gmd->fmd', weights, value_flat, preferred_element_type=jn...  8.14 us
    ppermute x7, starting transfers between devices, exchange_in_pairs(): outs.append(lax.ppermute(sent, axis, [(i, i ^ step) for i in range(peers)]))  7.77 us
    convert_element_type x2, local copies, waits for them, and re-layouts, project(): jnp.einsum('fpd,dc->fpc', source, weight, preferred_element_type=jnp.floa...  7.5 us
  transfers between devices with their start and end apart: 10, of which 4 were waited for; matrix products, arithmetic and copies ran while one was open for 17% of the time, Pallas kernels for 0%

profile of v1, /device:TPU:0, one launch (start us, length us, event | category | flops | bytes accessed | tf_op | source)
XLA Modules:
  0.0 314.2 jit_solution(8882902447370088988)
XLA Ops:
  6.5 0.0 copy-start
  6.5 0.0 copy-start.1
  6.5 4.7 %convert_reduce_fusion = f32[4,1024]{1,0:T(4,128)S(1)} fusion(bf16[4,1024,1024]{2,1,0:T(8,128)(2,1)} %param.5), kind=kLoop, calls=%fused_computation.3 | loop fusion | flops 8384512 | bytes 8404992 | tf_op jit(solution)/shard_map/reduce_sum | solution.py:35
  11.3 1.1 copy-done.1
  12.4 0.0 copy-start.4
  12.4 2.8 fusion.3
  15.2 0.0 copy-done.4
  15.2 0.0 copy-start.5
  15.2 5.1 %fusion.28 = bf16[4,1024,256]{2,1,0:T(8,128)(2,1)S(1)} fusion(bf16[4,1024,1024]{2,1,0:T(8,128)(2,1)} %param.5, f32[4,1024]{1,0:T(4,128)S(1)} %add_rsqrt_fusion, f32[4,1024]{1,0:T(4,128)S(1)} %broadcast_multiply_fusion, bf16[1024,256]{1,0:T(8,128)(2,1)S(1)} %copy-done.4), kind=kOutput, calls=%fused_computation.29 | convolution fusion | flops 2165309440 | bytes 11042816 | tf_op jit(solution)/shard_map/fpd,dc->fpc/dot_general | solution.py:42
  20.3 0.0 copy-start.3
  20.3 1.3 dynamic-slice_bitcast_fusion
  21.6 0.5 collective-permute-start
  22.1 2.5 collective-permute-start.1
  24.6 0.1 collective-permute-start.2
  24.7 1.8 collective-permute-start.3
  26.5 0.0 collective-permute-start.4
  26.5 0.0 copy-done.5
  26.5 5.0 %fusion.31 = bf16[4,1024,256]{2,1,0:T(8,128)(2,1)S(1)} fusion(bf16[4,1024,1024]{2,1,0:T(8,128)(2,1)} %param.5, f32[4,1024]{1,0:T(4,128)S(1)} %add_rsqrt_fusion, f32[4,1024]{1,0:T(4,128)S(1)} %broadcast_multiply_fusion, bf16[1024,256]{1,0:T(8,128)(2,1)S(1)} %copy-done.5), kind=kOutput, calls=%fused_computation.30 | convolution fusion | flops 2165309440 | bytes 11042816 | tf_op jit(solution)/shard_map/fpd,dc->fpc/dot_general | solution.py:42
  31.5 0.0 copy-done.3
  31.5 2.9 copy.18
  34.5 4.0 %all-to-all-start.1 = ((bf16[4,1024,256]{2,0,1:T(4,128)(2,1)}), bf16[4,1024,256]{2,0,1:T(4,128)(2,1)S(1)}, u32[]{:S(2)}, u32[]{:S(2)}) async-start(bf16[4,1024,256]{2,0,1:T(4,128)(2,1)} %copy.18), calls=%async_computation.1 | async-start | bytes 4194304 | tf_op jit(solution)/shard_map/all_to_all | solution.py:70
  38.4 6.1 %fusion.25 = bf16[4,1024,256]{2,1,0:T(8,128)(2,1)} fusion(bf16[4,1024,1024]{2,1,0:T(8,128)(2,1)} %param.5, f32[4,1024]{1,0:T(4,128)S(1)} %add_rsqrt_fusion, f32[4,1024]{1,0:T(4,128)S(1)} %broadcast_multiply_fusion, bf16[1024,256]{1,0:T(8,128)(2,1)} %param.8), kind=kOutput, calls=%fused_computation.28 | convolution fusion | flops 2165309440 | bytes 11042816 | tf_op jit(solution)/shard_map/fpd,dc->fpc/dot_general | solution.py:42
  44.5 1.7 bitcast_dynamic-update-slice_fusion.7
  46.2 4.6 %copy.16 = bf16[4,1024,256]{2,0,1:T(4,128)(2,1)} copy(bf16[4,1024,256]{2,1,0:T(8,128)(2,1)} %fusion.25) | data formatting | bytes 4194304 | tf_op jit(solution)/shard_map/convert_element_type | solution.py:42
  50.8 0.0 collective-permute-done
  50.8 2.9 collective-permute-start.5
  53.7 1.7 bitcast_dynamic-update-slice_fusion.6
  55.4 0.0 collective-permute-done.1
  55.4 0.0 collective-permute-start.6
  55.4 1.7 bitcast_dynamic-update-slice_fusion.5
  57.0 0.0 collective-permute-done.2
  57.0 0.7 bitcast_dynamic-update-slice_fusion.4
  57.8 0.0 collective-permute-done.3
  57.8 0.7 bitcast_dynamic-update-slice_fusion.3
  58.5 7.1 %all-to-all-done.1 = bf16[4,1024,256]{2,0,1:T(4,128)(2,1)S(1)} async-done(((bf16[4,1024,256]{2,0,1:T(4,128)(2,1)}), bf16[4,1024,256]{2,0,1:T(4,128)(2,1)S(1)}, u32[]{:S(2)}, u32[]{:S(2)}) %all-to-all-start.1) | async-done | bytes 2097184 | tf_op jit(solution)/shard_map/all_to_all | solution.py:70
  65.6 0.0 copy-start.2
  65.6 4.4 %all-to-all-start = ((bf16[4,1024,256]{2,0,1:T(4,128)(2,1)}), bf16[4,1024,256]{2,0,1:T(4,128)(2,1)}, u32[]{:S(2)}, u32[]{:S(2)}) async-start(bf16[4,1024,256]{2,0,1:T(4,128)(2,1)} %copy.16), calls=%async_computation | async-start | bytes 4194304 | tf_op jit(solution)/shard_map/all_to_all | solution.py:72
  70.0 0.2 reduce-scatter.2.cloned.1.call-start
  70.2 0.0 collective-permute-done.4
  70.2 0.7 bitcast_dynamic-update-slice_fusion.2
  70.9 0.4 collective-permute-done.5
  71.3 1.7 bitcast_dynamic-update-slice_fusion.1
  73.0 2.9 collective-permute-done.6
  75.9 0.0 copy-done.2
  75.9 1.6 bitcast_dynamic-update-slice_fusion
  77.6 2.3 gather_fusion
  79.8 3.3 %reshape_reshape.3 = bf16[32,512,64]{2,1,0:T(8,128)(2,1)} reshape(bf16[8,4,128,256]{3,2,1,0:T(8,128)(2,1)S(1)} %gather_fusion) | data formatting | bytes 4194304 | tf_op jit(solution)/shard_map/reshape;reshape | solution.py:51
  83.1 2.0 copy.37
  85.1 3.3 %reshape.61 = bf16[32,512,64]{2,1,0:T(8,128)(2,1)} reshape(bf16[8,4,128,256]{3,2,1,0:T(8,128)(2,1)S(1)} %bitcast.77) | data formatting | bytes 4194304 | tf_op jit(solution)/shard_map/reshape | solution.py:50
  88.3 8.3 %fusion.18 = f32[512,32,32]{2,1,0:T(8,128)S(1)} fusion(bf16[32,512,64]{2,1,0:T(8,128)(2,1)} %reshape.61, bf16[32,512,64]{2,1,0:T(8,128)(2,1)} %reshape_reshape.3), kind=kOutput, calls=%fused_computation.20 | convolution fusion | flops 67108864 | bytes 6291456 | tf_op jit(solution)/shard_map/fmd,gmd->fgm/dot_general | solution.py:53
  96.6 6.1 %fusion.40 = (f32[32,512]{0,1:T(8,128)S(1)}, f32[32,32,512]{0,1,2:T(8,128)}) fusion(f32[512,32,32]{2,1,0:T(8,128)S(1)} %fusion.18), kind=kOutput, calls=%fused_computation.56 | output fusion | flops 2097183 | bytes 4259840 | tf_op jit(solution)/shard_map/sub | solution.py:57
  102.8 0.0 all-to-all-done
  102.8 2.0 copy.38
  104.8 3.3 %reshape.59 = bf16[32,512,64]{2,1,0:T(8,128)(2,1)} reshape(bf16[8,4,128,256]{3,2,1,0:T(8,128)(2,1)S(1)} %bitcast.78) | data formatting | bytes 4194304 | tf_op jit(solution)/shard_map/reshape | solution.py:52
  108.0 8.1 %convert_bitcast_fusion = bf16[32,512,64]{2,0,1:T(8,128)(2,1)S(1)} fusion(f32[32,32,512]{0,1,2:T(8,128)} %get-tuple-element.13, f32[32,512]{0,1:T(8,128)S(1)} %get-tuple-element.12, bf16[32,512,64]{2,1,0:T(8,128)(2,1)} %reshape.59), kind=kOutput, calls=%fused_computation.23 | convolution fusion | flops 69206016 | bytes 6356992 | tf_op jit(solution)/shard_map/fgm,gmd->fmd/dot_general | solution.py:59
  116.2 3.6 %copy.24 = bf16[32,512,64]{2,1,0:T(8,128)(2,1)} copy(bf16[32,512,64]{2,0,1:T(8,128)(2,1)S(1)} %convert_bitcast_fusion) | data formatting | bytes 4194304 | tf_op jit(solution)/shard_map/convert_element_type | solution.py:60
  119.8 5.5 %reshape.62 = bf16[32,128,256]{2,1,0:T(8,128)(2,1)S(1)} reshape(bf16[32,512,64]{2,1,0:T(8,128)(2,1)} %copy.24) | data formatting | bytes 4194304 | tf_op jit(solution)/shard_map/reshape | solution.py:60
  125.3 0.0 copy-done
  125.3 5.6 %convolution_convert_fusion = bf16[32,128,1024]{2,1,0:T(8,128)(2,1)} fusion(bf16[32,128,256]{2,1,0:T(8,128)(2,1)S(1)} %reshape.62, bf16[256,1024]{1,0:T(8,128)(2,1)S(1)} %copy-done), kind=kOutput, calls=%fused_computation.14 | convolution fusion | flops 2151677952 | bytes 11010048 | tf_op jit(solution)/shard_map/fpc,cd->fpd/dot_general | solution.py:75
  130.9 0.0 reduce-scatter.2.cloned.1.call-update
  130.9 144.8 %reduce-scatter.2.cloned.1.call-done = bf16[32,128,256]{2,1,0:T(8,128)(2,1)} async-done(((bf16[32,128,1024]{2,1,0:T(8,128)(2,1)}), bf16[32,128,256]{2,1,0:T(8,128)(2,1)}) %reduce-scatter.2.cloned.1.call-update) | async-done | bytes 2097168 | tf_op jit(solution)/shard_map/reduce_scatter | solution.py:76
  275.7 30.2 %all_to_all.48 = bf16[32,128,256]{2,1,0:T(8,128)(2,1)S(1)} all-to-all(bf16[32,128,256]{2,1,0:T(8,128)(2,1)} %reduce-scatter.2.cloned.1.call-done), channel_id=1, replica_groups=mesh['seq'=8,'head'=4] {'seq'}, dimensions={0} | all-to-all | bytes 4194304 | tf_op jit(solution)/shard_map/all_to_all | solution.py:79
  305.9 1.5 copy.25
  (4 shorter events, 0.0 us)
Async XLA Ops:
  6.5 118.7 %copy-start = (bf16[256,1024]{1,0:T(8,128)(2,1)S(1)}, bf16[256,1024]{1,0:T(8,128)(2,1)}, u32[]{:S(2)}) copy-start(bf16[256,1024]{1,0:T(8,128)(2,1)} %param.9) | copy-start | bytes 1572868
  6.5 5.8 %copy-start.1 = (bf16[4,1024,1024]{2,1,0:T(8,128)(2,1)S(1)}, bf16[4,1024,1024]{2,1,0:T(8,128)(2,1)}, u32[]{:S(2)}) copy-start(bf16[4,1024,1024]{2,1,0:T(8,128)(2,1)} %param.5) | copy-start | bytes 25165828
  12.4 2.9 copy-start.4
  15.2 11.3 %copy-start.5 = (bf16[1024,256]{1,0:T(8,128)(2,1)S(1)}, bf16[1024,256]{1,0:T(8,128)(2,1)}, u32[]{:S(2)}) copy-start(bf16[1024,256]{1,0:T(8,128)(2,1)} %param.6) | copy-start | bytes 1572868
  20.3 11.2 %copy-start.3 = (bf16[4,1024,256]{2,1,0:T(8,128)(2,1)}, bf16[4,1024,256]{2,1,0:T(8,128)(2,1)S(1)}, u32[]{:S(2)}) copy-start(bf16[4,1024,256]{2,1,0:T(8,128)(2,1)S(1)} %fusion.28) | copy-start | bytes 6291460
  21.6 29.1 %collective-permute-start = (bf16[4,128,256]{2,1,0:T(8,128)(2,1)}, bf16[4,128,256]{2,1,0:T(8,128)(2,1)}, u32[]{:S(2)}, u32[]{:S(2)}) collective-permute-start(bf16[4,128,256]{2,1,0:T(8,128)(2,1)} %get-tuple-element.11), channel_id=1, source_target_pairs={{0,4},{4,0},{8,12},{12,8},{16,20},{20,16},{24,28},{28,24},{1,5},{5... | collective-permute-start | bytes 786440 | tf_op jit(solution)/shard_map/ppermute | solution.py:28
  22.1 33.2 %collective-permute-start.1 = (bf16[4,128,256]{2,1,0:T(8,128)(2,1)}, bf16[4,128,256]{2,1,0:T(8,128)(2,1)}, u32[]{:S(2)}, u32[]{:S(2)}) collective-permute-start(bf16[4,128,256]{2,1,0:T(8,128)(2,1)} %get-tuple-element.10), channel_id=1, source_target_pairs={{0,8},{4,12},{8,0},{12,4},{16,24},{20,28},{24,16},{28,20},{1,9},{5... | collective-permute-start | bytes 786440 | tf_op jit(solution)/shard_map/ppermute | solution.py:28
  24.6 32.4 %collective-permute-start.2 = (bf16[4,128,256]{2,1,0:T(8,128)(2,1)}, bf16[4,128,256]{2,1,0:T(8,128)(2,1)S(1)}, u32[]{:S(2)}, u32[]{:S(2)}) collective-permute-start(bf16[4,128,256]{2,1,0:T(8,128)(2,1)} %get-tuple-element.9), channel_id=1, source_target_pairs={{0,12},{4,8},{8,4},{12,0},{16,28},{20,24},{24,20},{28,16},{1,13},{... | collective-permute-start | bytes 786440 | tf_op jit(solution)/shard_map/ppermute | solution.py:28
  24.7 33.0 %collective-permute-start.3 = (bf16[4,128,256]{2,1,0:T(8,128)(2,1)}, bf16[4,128,256]{2,1,0:T(8,128)(2,1)S(1)}, u32[]{:S(2)}, u32[]{:S(2)}) collective-permute-start(bf16[4,128,256]{2,1,0:T(8,128)(2,1)} %get-tuple-element.8), channel_id=1, source_target_pairs={{0,16},{4,20},{8,24},{12,28},{16,0},{20,4},{24,8},{28,12},{1,17},{... | collective-permute-start | bytes 786440 | tf_op jit(solution)/shard_map/ppermute | solution.py:28
  26.5 43.7 %collective-permute-start.4 = (bf16[4,128,256]{2,1,0:T(8,128)(2,1)}, bf16[4,128,256]{2,1,0:T(8,128)(2,1)S(1)}, u32[]{:S(2)}, u32[]{:S(2)}) collective-permute-start(bf16[4,128,256]{2,1,0:T(8,128)(2,1)} %get-tuple-element.7), channel_id=1, source_target_pairs={{0,20},{4,16},{8,28},{12,24},{16,4},{20,0},{24,12},{28,8},{1,21},{... | collective-permute-start | bytes 786440 | tf_op jit(solution)/shard_map/ppermute | solution.py:28
  34.5 31.1 %all-to-all-start.1 = ((bf16[4,1024,256]{2,0,1:T(4,128)(2,1)}), bf16[4,1024,256]{2,0,1:T(4,128)(2,1)S(1)}, u32[]{:S(2)}, u32[]{:S(2)}) async-start(bf16[4,1024,256]{2,0,1:T(4,128)(2,1)} %copy.18), calls=%async_computation.1 | async-start | bytes 4194304 | tf_op jit(solution)/shard_map/all_to_all | solution.py:70
  50.8 20.6 %collective-permute-start.5 = (bf16[4,128,256]{2,1,0:T(8,128)(2,1)}, bf16[4,128,256]{2,1,0:T(8,128)(2,1)}, u32[]{:S(2)}, u32[]{:S(2)}) collective-permute-start(bf16[4,128,256]{2,1,0:T(8,128)(2,1)} %get-tuple-element.6), channel_id=1, source_target_pairs={{0,24},{4,28},{8,16},{12,20},{16,8},{20,12},{24,0},{28,4},{1,25},{... | collective-permute-start | bytes 786440 | tf_op jit(solution)/shard_map/ppermute | solution.py:28
  55.4 20.5 %collective-permute-start.6 = (bf16[4,128,256]{2,1,0:T(8,128)(2,1)}, bf16[4,128,256]{2,1,0:T(8,128)(2,1)}, u32[]{:S(2)}, u32[]{:S(2)}) collective-permute-start(bf16[4,128,256]{2,1,0:T(8,128)(2,1)} %get-tuple-element.5), channel_id=1, source_target_pairs={{0,28},{4,24},{8,20},{12,16},{16,12},{20,8},{24,4},{28,0},{1,29},{... | collective-permute-start | bytes 786440 | tf_op jit(solution)/shard_map/ppermute | solution.py:28
  65.6 10.3 %copy-start.2 = (bf16[4,1024,256]{2,0,1:T(4,128)(2,1)}, bf16[4,1024,256]{2,0,1:T(4,128)(2,1)S(1)}, u32[]{:S(2)}) copy-start(bf16[4,1024,256]{2,0,1:T(4,128)(2,1)S(1)} %all-to-all-done.1) | copy-start | bytes 6291460
  65.6 37.2 %all-to-all-start = ((bf16[4,1024,256]{2,0,1:T(4,128)(2,1)}), bf16[4,1024,256]{2,0,1:T(4,128)(2,1)}, u32[]{:S(2)}, u32[]{:S(2)}) async-start(bf16[4,1024,256]{2,0,1:T(4,128)(2,1)} %copy.16), calls=%async_computation | async-start | bytes 4194304 | tf_op jit(solution)/shard_map/all_to_all | solution.py:72
  70.0 205.7 %reduce-scatter.2.cloned.1.call-start = ((), (), s32[]{:S(2)}) async-start(), calls=%async_computation.4 | async-start | bytes 10485760 | tf_op jit(solution)/shard_map/reduce_scatter | solution.py:76
Sparse Core Ops, SparseCore 0:
  131.0 144.6 reduce-scatter.1
